TPU v7x, 32 devices: a whole 2x2x4 slice. The times are simulated.
32 devices in a mesh: section: 4 (over y, x), row: 8 (over z, core).
Axes of the slice: x: 2, y: 2, z: 4, core: 2. Of those that a mesh axis runs over, the one named last changes fastest.
Arguments:
- omega: bfloat16 [2048, 8192], P('section', 'row'), may hold values from -0.5 to 0.5
- basis: bfloat16 [8192, 1024], P('row', 'section'), may hold values from -6 to 6
- vectors: bfloat16 [4, 8192], P(None, 'row'), may hold values from -6 to 6
Outputs:
- ortho: float32 [4, 8192], P(None, ('row', 'section'))
- coeffs: float32 [4, 1024], P(None, 'section')
All inputs are finite; a program needn't handle non-finite values.
Results may differ from a plain program's by a relative error of at most 0.0021.
Values may be sent and summed in bfloat16 or wider, within the bound.
A program may use at most 64 MiB of HBM per device.

v0:
```python
import jax
import jax.numpy as jnp
from jax import lax
from jax.sharding import PartitionSpec as P


def from_behind(value, axis, steps):
    count = lax.axis_size(axis)
    initial, last = (max(0, -steps), min(count, count - steps))
    return lax.ppermute(value, axis, [(source, source + steps) for source in range(initial, last)])


def from_root(value, axis, source):
    kept = jnp.where(lax.axis_index(axis) == source, value, 0).astype(value.dtype)
    return lax.psum(kept, axis)


def lower_solve(factor, right):
    return lax.linalg.triangular_solve(factor, right, left_side=True, lower=True, transpose_a=False)


def factor_solve(factor, right):
    half = lower_solve(factor, right)
    return lax.linalg.triangular_solve(factor, half, left_side=True, lower=True, transpose_a=True)


def body(omega, basis, vectors):
    hi = lax.Precision.HIGHEST
    sections = lax.axis_size("section")
    my_section = lax.axis_index("section")
    whole = lax.all_gather(omega, "section", axis=0, tiled=True)
    sketch = lax.psum_scatter(
        jnp.dot(whole, basis, preferred_element_type=jnp.float32),
        "row",
        scatter_dimension=0,
        tiled=True,
    )
    probe_term = lax.dot_general(
        vectors, whole, (((1,), (1,)), ((), ())), preferred_element_type=jnp.float32
    )
    probe = lax.psum_scatter(probe_term, "row", scatter_dimension=1, tiled=True)
    gram = lax.psum(jnp.dot(sketch.T, sketch, precision=hi), "row")
    factor = jnp.linalg.cholesky(gram)

    def project(current):
        inner = jnp.dot(current, sketch, precision=hi)
        inner = lax.psum(inner, "row")
        coef = factor_solve(factor, inner.T).T
        return (coef, current - jnp.dot(coef, sketch.T, precision=hi))

    def advance(step, carry):
        current, kept = carry
        coef, moved = project(current)
        active = my_section == step
        kept = jnp.where(active, coef, kept)
        moved = jnp.where(active, moved, current)
        return (from_behind(moved, "section", 1), kept)

    start_coef = jnp.zeros((vectors.shape[0], basis.shape[1]), jnp.float32)
    probe, kept = lax.fori_loop(0, sections - 1, advance, (probe, start_coef))
    coef, moved = project(probe)
    finished = my_section == sections - 1
    kept = jnp.where(finished, coef, kept)
    final = from_root(moved, "section", sections - 1)
    rounded = kept.astype(jnp.bfloat16)
    own_term = lax.dot_general(
        rounded, basis, (((1,), (1,)), ((), ())), preferred_element_type=jnp.float32
    )
    removed = lax.psum_scatter(own_term, "section", scatter_dimension=1, tiled=True)
    width = removed.shape[1]
    mine = lax.dynamic_slice_in_dim(vectors, my_section * width, width, 1)
    remain = mine.astype(jnp.float32) - removed
    small = lax.psum(jnp.dot(final, final.T, precision=hi), "row")
    lower = jnp.linalg.cholesky(small)
    ortho = lower_solve(lower, remain)
    return (ortho, kept)


def solution(mesh):
    return jax.shard_map(
        body,
        mesh=mesh,
        in_specs=(P("section", "row"), P("row", "section"), P(None, "row")),
        out_specs=(P(None, ("row", "section")), P(None, "section")),
        check_vma=False,
    )
```

profile of v0, /device:TPU:0, one launch (start us, length us, event | category | flops | bytes accessed | tf_op | source)
XLA Modules:
  0.0 442.4 jit_solution(2750653464107480190)
XLA Ops:
  8.0 57.2 %all-gather.2.cloned.1.call-done = bf16[2048,1024]{1,0:T(8,128)(2,1)} async-done(((bf16[512,1024]{1,0:T(8,128)(2,1)}), bf16[2048,1024]{1,0:T(8,128)(2,1)}) %all-gather.2.cloned.1.call-update) | async-done | bytes 4194320 | tf_op jit(solution)/shard_map/all_gather | solution.py:31
  65.2 4.8 %fusion.36 = f32[2048,256]{1,0:T(8,128)} fusion(bf16[2048,1024]{1,0:T(8,128)(2,1)} %all-gather.2.cloned.1.call-done, bf16[1024,256]{1,0:T(8,128)(2,1)S(1)} %copy-done), kind=kOutput, calls=%fused_computation.78 | convolution fusion | flops 1073741824 | bytes 6815744 | tf_op jit(solution)/shard_map/dot_general | solution.py:33
  70.0 4.4 convolution_bitcast_fusion
  74.5 31.6 %reduce-scatter.8.cloned.1.call-done = f32[256,256]{1,0:T(8,128)} async-done(((f32[2048,256]{1,0:T(8,128)}), f32[256,256]{1,0:T(8,128)}) %reduce-scatter.8.cloned.1.call-update) | async-done | bytes 262160 | tf_op jit(solution)/shard_map/reduce_scatter | solution.py:32
  106.1 2.4 fusion.37
  108.8 30.9 %reduce-scatter.10.cloned.1.call-done = f32[256,4]{1,0:T(8,128)} async-done(((f32[2048,4]{1,0:T(8,128)}), f32[256,4]{1,0:T(8,128)}) %reduce-scatter.10.cloned.1.call-update) | async-done | bytes 4112
  140.7 54.8 %all-reduce.3.cloned.1.call-done = f32[256,256]{0,1:T(8,128)} async-done(((f32[256,256]{0,1:T(8,128)}), f32[256,256]{0,1:T(8,128)}) %all-reduce.3.cloned.1.call-update) | async-done | bytes 262160 | tf_op jit(solution)/shard_map/psum | solution.py:42
  197.6 11.7 %cholesky.64 = f32[128,128]{1,0:T(8,128)S(1)} custom-call(f32[128,128]{1,0:T(8,128)S(1)} %cholesky.153), custom_call_target="Cholesky" | custom-call | tf_op jit(solution)/shard_map/jit(cholesky)/cholesky | solution.py:43
  209.4 9.8 %custom-call.23 = f32[1,128,128]{1,2,0:T(8,128)S(1)} custom-call(f32[1,128,128]{2,1,0:T(8,128)S(1)} %get-tuple-element.206), custom_call_target="InvertDiagBlocksLowerTriangular" | custom-call | tf_op jit(solution)/shard_map/jit(cholesky)/cholesky | solution.py:43
  219.7 11.7 %cholesky.131 = f32[128,128]{1,0:T(8,128)S(1)} custom-call(f32[128,128]{1,0:T(8,128)S(1)} %convolution_subtract_fusion.3), custom_call_target="Cholesky" | custom-call | tf_op jit(solution)/shard_map/jit(cholesky)/cholesky | solution.py:43
  233.5 4.2 while.27
  234.4 1.3 bitcast_dynamic-update-slice_fusion.4
  236.4 1.3 bitcast_dynamic-update-slice_fusion.4
  237.8 19.7 %custom-call.31 = f32[2,128,128]{1,2,0:T(8,128)S(1)} custom-call(f32[2,128,128]{2,1,0:T(8,128)S(1)} %get-tuple-element.168), custom_call_target="InvertDiagBlocksLowerTriangular" | custom-call | tf_op jit(solution)/shard_map/triangular_solve/custom-call.4 | solution.py:24
  257.4 133.4 %while.26 = (s32[]{:T(128)}, f32[4,256]{1,0:T(4,128)S(1)}, f32[4,256]{1,0:T(4,128)S(1)}, s32[]{:T(128)}, f32[256,256]{1,0:T(8,128)S(1)}, /*index=5*/f32[256,256]{1,0:T(8,128)S(1)}, s32[]{:T(128)}, s32[]{:T(128)}, s32[]{:T(128)}) while((s32[]{:T(128)}, f32[4,256]{1,0:T(4,128)S(1)}, f32[4,256]{1,0:T(4,128)S(1)}, s32[]{:T(128)}, ...), condition=%wide.region_9.12_spmd.clone, body=%wide.region_7.0_spmd.clone.sunk | while | flops 11149320 | bytes 1659231 | solution.py:60
  257.6 4.1 while.28
  261.6 19.7 %custom-call.37 = f32[2,128,128]{1,2,0:T(8,128)S(1)} custom-call(f32[2,128,128]{2,1,0:T(8,128)S(1)} %get-tuple-element.303), custom_call_target="InvertDiagBlocksLowerTriangular" | custom-call | tf_op jit(solution)/shard_map/while/body/eval_jaxpr/triangular_solve/custom-call.4 | solution.py:24
  281.5 13.7 %psum.45 = f32[256,4]{0,1:T(4,128)S(1)} all-reduce(f32[256,4]{0,1:T(4,128)S(1)} %fusion.99), channel_id=1, replica_groups=mesh['section'=4,'row'=8] {'row'}, use_global_device_ids=true, to_apply=%region_8.8 | all-reduce | flops 1024 | bytes 8192 | tf_op jit(solution)/shard_map/while/body/eval_jaxpr/psum | solution.py:47
  296.7 3.4 collective-permute-start
  301.5 4.1 while.28
  302.2 1.3 bitcast_dynamic-update-slice_fusion.5
  304.2 1.3 bitcast_dynamic-update-slice_fusion.5
  305.6 19.7 %custom-call.37 = f32[2,128,128]{1,2,0:T(8,128)S(1)} custom-call(f32[2,128,128]{2,1,0:T(8,128)S(1)} %get-tuple-element.303), custom_call_target="InvertDiagBlocksLowerTriangular" | custom-call | tf_op jit(solution)/shard_map/while/body/eval_jaxpr/triangular_solve/custom-call.4 | solution.py:24
  325.5 13.6 %psum.45 = f32[256,4]{0,1:T(4,128)S(1)} all-reduce(f32[256,4]{0,1:T(4,128)S(1)} %fusion.99), channel_id=1, replica_groups=mesh['section'=4,'row'=8] {'row'}, use_global_device_ids=true, to_apply=%region_8.8 | all-reduce | flops 1024 | bytes 8192 | tf_op jit(solution)/shard_map/while/body/eval_jaxpr/psum | solution.py:47
  340.6 4.2 collective-permute-start
  346.2 4.1 while.28
  350.3 19.7 %custom-call.37 = f32[2,128,128]{1,2,0:T(8,128)S(1)} custom-call(f32[2,128,128]{2,1,0:T(8,128)S(1)} %get-tuple-element.303), custom_call_target="InvertDiagBlocksLowerTriangular" | custom-call | tf_op jit(solution)/shard_map/while/body/eval_jaxpr/triangular_solve/custom-call.4 | solution.py:24
  370.2 13.6 %psum.45 = f32[256,4]{0,1:T(4,128)S(1)} all-reduce(f32[256,4]{0,1:T(4,128)S(1)} %fusion.99), channel_id=1, replica_groups=mesh['section'=4,'row'=8] {'row'}, use_global_device_ids=true, to_apply=%region_8.8 | all-reduce | flops 1024 | bytes 8192 | tf_op jit(solution)/shard_map/while/body/eval_jaxpr/psum | solution.py:47
  385.2 4.3 collective-permute-start
  391.1 13.6 %psum.40 = f32[256,4]{0,1:T(4,128)S(1)} all-reduce(f32[256,4]{0,1:T(4,128)S(1)} %fusion.38), channel_id=1, replica_groups=mesh['section'=4,'row'=8] {'row'}, use_global_device_ids=true, to_apply=%region_10.13 | all-reduce | flops 1024 | bytes 8192 | tf_op jit(solution)/shard_map/psum | solution.py:47
  407.2 11.0 %psum.41 = f32[4,256]{1,0:T(4,128)S(1)} all-reduce(f32[4,256]{1,0:T(4,128)S(1)} %fusion.10), channel_id=1, replica_groups=mesh['section'=4,'row'=8] {'section'}, use_global_device_ids=true, to_apply=%region_11.14 | all-reduce | flops 1024 | bytes 8192 | tf_op jit(solution)/shard_map/psum | solution.py:15
  418.3 13.6 %psum.42 = f32[4,4]{0,1:T(4,128)S(1)} all-reduce(f32[4,4]{0,1:T(4,128)S(1)} %fusion.39), channel_id=1, replica_groups=mesh['section'=4,'row'=8] {'row'}, use_global_device_ids=true, to_apply=%region_12.15 | all-reduce | flops 16 | bytes 128 | tf_op jit(solution)/shard_map/psum | solution.py:73
  (116 shorter events, 32.2 us)
Async XLA Ops:
  7.2 58.0 %copy-start = (bf16[1024,256]{1,0:T(8,128)(2,1)S(1)}, bf16[1024,256]{1,0:T(8,128)(2,1)}, u32[]{:S(2)}) copy-start(bf16[1024,256]{1,0:T(8,128)(2,1)} %param.10) | copy-start | bytes 1572868
  7.2 58.0 %all-gather.2.cloned.1.call-start = ((), (), s32[]{:S(2)}) async-start(), calls=%async_computation.3 | async-start | bytes 5242880 | tf_op jit(solution)/shard_map/all_gather | solution.py:31
  7.9 62.1 %copy-start.3 = (bf16[4,1024]{1,0:T(4,128)(2,1)S(1)}, bf16[4,1024]{1,0:T(4,128)(2,1)}, u32[]{:S(2)}) copy-start(bf16[4,1024]{1,0:T(4,128)(2,1)} %param.11) | copy-start | bytes 24580
  7.9 98.2 %reduce-scatter.8.cloned.1.call-start = ((), (), s32[]{:S(2)}) async-start(), calls=%async_computation.4 | async-start | bytes 2359296 | tf_op jit(solution)/shard_map/reduce_scatter | solution.py:32
  70.0 69.7 %reduce-scatter.10.cloned.1.call-start = ((), (), s32[]{:S(2)}) async-start(), calls=%async_computation.6 | async-start | bytes 1179648
  74.5 121.0 %all-reduce.3.cloned.1.call-start = ((), (), s32[]{:S(2)}) async-start(), calls=%async_computation.5 | async-start | bytes 524288 | tf_op jit(solution)/shard_map/psum | solution.py:42
  106.1 151.3 %copy-start.1 = (f32[256,256]{1,0:T(8,128)S(1)}, f32[256,256]{1,0:T(8,128)}, u32[]{:S(2)}) copy-start(f32[256,256]{1,0:T(8,128)} %reduce-scatter.8.cloned.1.call-done) | copy-start | bytes 786436
  108.5 325.5 %reduce-scatter.12.cloned.1.call-start = ((), (), s32[]{:S(2)}) async-start(), calls=%async_computation.7 | async-start | bytes 655360
  296.7 4.7 %collective-permute-start = (f32[4,256]{1,0:T(4,128)S(1)}, f32[4,256]{1,0:T(4,128)S(1)}, u32[]{:S(2)}, u32[]{:S(2)}) collective-permute-start(f32[4,256]{1,0:T(4,128)S(1)} %fusion.104), channel_id=1, source_target_pairs={{0,8},{8,16},{16,24},{1,9},{9,17},{17,25},{2,10},{10,18},{18,26},{... | collective-permute-start | bytes 12296 | tf_op jit(solution)/shard_map/while/body/eval_jaxpr/ppermute | solution.py:10
  340.6 5.6 %collective-permute-start = (f32[4,256]{1,0:T(4,128)S(1)}, f32[4,256]{1,0:T(4,128)S(1)}, u32[]{:S(2)}, u32[]{:S(2)}) collective-permute-start(f32[4,256]{1,0:T(4,128)S(1)} %fusion.104), channel_id=1, source_target_pairs={{0,8},{8,16},{16,24},{1,9},{9,17},{17,25},{2,10},{10,18},{18,26},{... | collective-permute-start | bytes 12296 | tf_op jit(solution)/shard_map/while/body/eval_jaxpr/ppermute | solution.py:10
  385.2 5.6 %collective-permute-start = (f32[4,256]{1,0:T(4,128)S(1)}, f32[4,256]{1,0:T(4,128)S(1)}, u32[]{:S(2)}, u32[]{:S(2)}) collective-permute-start(f32[4,256]{1,0:T(4,128)S(1)} %fusion.104), channel_id=1, source_target_pairs={{0,8},{8,16},{16,24},{1,9},{9,17},{17,25},{2,10},{10,18},{18,26},{... | collective-permute-start | bytes 12296 | tf_op jit(solution)/shard_map/while/body/eval_jaxpr/ppermute | solution.py:10
  405.9 30.0 %copy-start.2 = (f32[4,256]{1,0:T(4,128)}, f32[4,256]{1,0:T(4,128)S(1)}, u32[]{:S(2)}) copy-start(f32[4,256]{1,0:T(4,128)S(1)} %bitcast_select_fusion.1) | copy-start | bytes 12292
Sparse Core Ops, SparseCore 0:
  9.8 55.2 all-gather.1
  70.1 35.9 reduce-scatter.7
  108.4 31.2 reduce-scatter.9
  141.9 53.5 all-reduce.2
  407.1 25.7 reduce-scatter.11
where the time goes:
time: 443 us; the launch traced here: 442 us
  waiting for transfers between devices  179 us (40%)
  other arithmetic  116 us (26%)
  blocking collectives  79.1 us (18%)
  matrix products  20.6 us (5%)
  local copies, waits for them, and re-layouts  19.6 us (4%)
  between operations  15.2 us (3%)
  starting transfers between devices  12.4 us (3%)
    another operation x16, other arithmetic, factor_solve(): lax.linalg.triangular_solve(factor, half, left_side=True, lower=True, tra...  78.8 us
    all_gather x1, waiting for transfers between devices, body(): whole = lax.all_gather(omega, 'section', axis=0, tiled=True)  57.2 us
    psum x1, waiting for transfers between devices, body(): gram = lax.psum(jnp.dot(sketch.T, sketch, precision=hi), 'row')  54.8 us
    psum x4, blocking collectives, project(): inner = lax.psum(inner, 'row')  54.5 us
    another operation x6, other arithmetic, body(): factor = jnp.linalg.cholesky(gram)  34 us
    unnamed x7, waiting for transfers between devices  31.7 us
    reduce_scatter x1, waiting for transfers between devices, body(): lax.psum_scatter(jnp.dot(whole, basis, preferred_element_type=jnp.float32...  31.6 us
    another operation x28, local copies, waits for them, and re-layouts, factor_solve(): lax.linalg.triangular_solve(factor, half, left_side=True, lower=True, tra...  16.4 us
  transfers between devices with their start and end apart: 8, of which 7 were waited for; matrix products, arithmetic and copies ran while one was open for 2% of the time, Pallas kernels for 0%

commit v1 on v0

--- a/solution.py
+++ b/solution.py
@@ -2,6 +2,16 @@
 import jax.numpy as jnp
 from jax import lax
 from jax.sharding import PartitionSpec as P
+
+
+def around_the_ring(x, axis, dim):
+    size = lax.axis_size(axis)
+    moving, pieces = (x, [x])
+    for _ in range(size - 1):
+        moving = lax.ppermute(moving, axis, [(i, (i + 1) % size) for i in range(size)])
+        pieces.insert(0, moving)
+    line = jnp.concatenate(pieces, axis=dim)
+    return jnp.roll(line, (lax.axis_index(axis) + 1) * x.shape[dim], axis=dim)
 
 
 def from_behind(value, axis, steps):
@@ -28,7 +38,7 @@
     hi = lax.Precision.HIGHEST
     sections = lax.axis_size("section")
     my_section = lax.axis_index("section")
-    whole = lax.all_gather(omega, "section", axis=0, tiled=True)
+    whole = around_the_ring(omega, "section", 0)
     sketch = lax.psum_scatter(
         jnp.dot(whole, basis, preferred_element_type=jnp.float32),
         "row",

time: 443 us -> 478 us (1.079)
  waiting for transfers between devices: 179 us -> 194 us
  local copies, waits for them, and re-layouts: 19.6 us -> 30.9 us
    ppermute x0 -> x3, waiting for transfers between devices: none -> 73.6 us  [around_the_ring(): lax.ppermute(moving, axis, [(i, (i + 1) % size) for i in range(size)])]
    all_gather x1 -> x0, waiting for transfers between devices: 57.2 us -> none  [body(): whole = lax.all_gather(omega, 'section', axis=0, tiled=True)]
    unnamed x10 -> x20, local copies, waits for them, and re-layouts: 2 us -> 13.2 us
    unnamed x7 -> x6, waiting for transfers between devices: 31.7 us -> 30.9 us
  transfers between devices with their start and end apart: 8 -> 10, of which waited for: 7 -> 9; matrix products, arithmetic and copies ran while one was open for 2% -> 2% of each run, Pallas kernels for 0% -> 0%
where the time goes in v1:
time: 478 us; the launch traced here: 477 us
  waiting for transfers between devices  194 us (41%)
  other arithmetic  116 us (24%)
  blocking collectives  79.1 us (17%)
  local copies, waits for them, and re-layouts  30.9 us (6%)
  matrix products  25.1 us (5%)
  starting transfers between devices  16.1 us (3%)
  between operations  15.2 us (3%)
    another operation x16, other arithmetic, factor_solve(): lax.linalg.triangular_solve(factor, half, left_side=True, lower=True, tra...  78.8 us
    ppermute x3, waiting for transfers between devices, around_the_ring(): lax.ppermute(moving, axis, [(i, (i + 1) % size) for i in range(size)])  73.6 us
    psum x1, waiting for transfers between devices, body(): gram = lax.psum(jnp.dot(sketch.T, sketch, precision=hi), 'row')  54.9 us
    psum x4, blocking collectives, project(): inner = lax.psum(inner, 'row')  54.6 us
    another operation x6, other arithmetic, body(): factor = jnp.linalg.cholesky(gram)  34 us
    reduce_scatter x1, waiting for transfers between devices, body(): lax.psum_scatter(jnp.dot(whole, basis, preferred_element_type=jnp.float32...  31.2 us
    unnamed x6, waiting for transfers between devices  30.9 us
    another operation x28, local copies, waits for them, and re-layouts, factor_solve(): lax.linalg.triangular_solve(factor, half, left_side=True, lower=True, tra...  16.4 us
  transfers between devices with their start and end apart: 10, of which 9 were waited for; matrix products, arithmetic and copies ran while one was open for 2% of the time, Pallas kernels for 0%

profile of v1, /device:TPU:0, one launch (start us, length us, event | category | flops | bytes accessed | tf_op | source)
XLA Modules:
  0.0 477.2 jit_solution(10943322785466974252)
XLA Ops:
  7.2 3.0 collective-permute-start.1
  10.3 24.3 %collective-permute-done.1 = bf16[512,1024]{1,0:T(8,128)(2,1)S(1)} collective-permute-done((bf16[512,1024]{1,0:T(8,128)(2,1)}, bf16[512,1024]{1,0:T(8,128)(2,1)S(1)}, u32[]{:S(2)}, u32[]{:S(2)}) %collective-permute-start.1) | collective-permute-done | bytes 1048608 | tf_op jit(solution)/shard_map/ppermute | solution.py:11
  35.4 24.5 %collective-permute-done.2 = bf16[512,1024]{1,0:T(8,128)(2,1)} collective-permute-done((bf16[512,1024]{1,0:T(8,128)(2,1)S(1)}, bf16[512,1024]{1,0:T(8,128)(2,1)}, u32[]{:S(2)}, u32[]{:S(2)}) %collective-permute-start.2) | collective-permute-done | bytes 1048608 | tf_op jit(solution)/shard_map/ppermute | solution.py:11
  59.9 24.7 %collective-permute-done.3 = bf16[512,1024]{1,0:T(8,128)(2,1)} collective-permute-done((bf16[512,1024]{1,0:T(8,128)(2,1)}, bf16[512,1024]{1,0:T(8,128)(2,1)}, u32[]{:S(2)}, u32[]{:S(2)}) %collective-permute-start.3) | collective-permute-done | bytes 1048608 | tf_op jit(solution)/shard_map/ppermute | solution.py:11
  91.4 3.2 copy-done.2
  94.6 2.7 fusion.10
  97.3 3.4 fusion.14
  102.2 31.2 %reduce-scatter.8.cloned.1.call-done = f32[256,256]{1,0:T(8,128)} async-done(((f32[2048,256]{1,0:T(8,128)}), f32[256,256]{1,0:T(8,128)}) %reduce-scatter.8.cloned.1.call-update) | async-done | bytes 262160 | tf_op jit(solution)/shard_map/reduce_scatter | solution.py:42
  133.3 2.3 fusion.45
  135.9 30.9 %reduce-scatter.10.cloned.1.call-done = f32[256,4]{1,0:T(8,128)} async-done(((f32[2048,4]{1,0:T(8,128)}), f32[256,4]{1,0:T(8,128)}) %reduce-scatter.10.cloned.1.call-update) | async-done | bytes 4112
  167.8 54.9 %all-reduce.3.cloned.1.call-done = f32[256,256]{0,1:T(8,128)} async-done(((f32[256,256]{0,1:T(8,128)}), f32[256,256]{0,1:T(8,128)}) %all-reduce.3.cloned.1.call-update) | async-done | bytes 262160 | tf_op jit(solution)/shard_map/psum | solution.py:52
  224.8 11.7 %cholesky.64 = f32[128,128]{1,0:T(8,128)S(1)} custom-call(f32[128,128]{1,0:T(8,128)S(1)} %cholesky.153), custom_call_target="Cholesky" | custom-call | tf_op jit(solution)/shard_map/jit(cholesky)/cholesky | solution.py:53
  236.6 9.8 %custom-call.23 = f32[1,128,128]{1,2,0:T(8,128)S(1)} custom-call(f32[1,128,128]{2,1,0:T(8,128)S(1)} %get-tuple-element.206), custom_call_target="InvertDiagBlocksLowerTriangular" | custom-call | tf_op jit(solution)/shard_map/jit(cholesky)/cholesky | solution.py:53
  246.9 11.7 %cholesky.131 = f32[128,128]{1,0:T(8,128)S(1)} custom-call(f32[128,128]{1,0:T(8,128)S(1)} %convolution_subtract_fusion.3), custom_call_target="Cholesky" | custom-call | tf_op jit(solution)/shard_map/jit(cholesky)/cholesky | solution.py:53
  260.7 4.2 while.27
  265.0 19.7 %custom-call.31 = f32[2,128,128]{1,2,0:T(8,128)S(1)} custom-call(f32[2,128,128]{2,1,0:T(8,128)S(1)} %get-tuple-element.168), custom_call_target="InvertDiagBlocksLowerTriangular" | custom-call | tf_op jit(solution)/shard_map/triangular_solve/custom-call.4 | solution.py:34
  284.7 139.1 %while.26 = (s32[]{:T(128)}, f32[4,256]{1,0:T(4,128)S(1)}, f32[4,256]{1,0:T(4,128)S(1)}, s32[]{:T(128)}, f32[256,256]{1,0:T(8,128)}, /*index=5*/f32[256,256]{1,0:T(8,128)S(1)}, s32[]{:T(128)}, s32[]{:T(128)}, s32[]{:T(128)}) while((s32[]{:T(128)}, f32[4,256]{1,0:T(4,128)S(1)}, f32[4,256]{1,0:T(4,128)S(1)}, s32[]{:T(128)}, ...), condition=%wide.region_9.12_spmd.clone, body=%wide.region_7.11_spmd.clone.sunk | while | flops 11149320 | bytes 1659231 | solution.py:70
  284.8 4.1 while.28
  288.9 19.7 %custom-call.39 = f32[2,128,128]{1,2,0:T(8,128)S(1)} custom-call(f32[2,128,128]{2,1,0:T(8,128)S(1)} %get-tuple-element.303), custom_call_target="InvertDiagBlocksLowerTriangular" | custom-call | tf_op jit(solution)/shard_map/while/body/eval_jaxpr/triangular_solve/custom-call.4 | solution.py:34
  309.7 13.7 %psum.45 = f32[256,4]{0,1:T(4,128)S(1)} all-reduce(f32[256,4]{0,1:T(4,128)S(1)} %fusion.105), channel_id=1, replica_groups=mesh['section'=4,'row'=8] {'row'}, use_global_device_ids=true, to_apply=%region_8.8 | all-reduce | flops 1024 | bytes 8192 | tf_op jit(solution)/shard_map/while/body/eval_jaxpr/psum | solution.py:57
  325.8 3.4 collective-permute-start
  330.6 4.1 while.28
  334.7 19.7 %custom-call.39 = f32[2,128,128]{1,2,0:T(8,128)S(1)} custom-call(f32[2,128,128]{2,1,0:T(8,128)S(1)} %get-tuple-element.303), custom_call_target="InvertDiagBlocksLowerTriangular" | custom-call | tf_op jit(solution)/shard_map/while/body/eval_jaxpr/triangular_solve/custom-call.4 | solution.py:34
  355.6 13.6 %psum.45 = f32[256,4]{0,1:T(4,128)S(1)} all-reduce(f32[256,4]{0,1:T(4,128)S(1)} %fusion.105), channel_id=1, replica_groups=mesh['section'=4,'row'=8] {'row'}, use_global_device_ids=true, to_apply=%region_8.8 | all-reduce | flops 1024 | bytes 8192 | tf_op jit(solution)/shard_map/while/body/eval_jaxpr/psum | solution.py:57
  371.6 4.2 collective-permute-start
  377.2 4.1 while.28
  381.3 19.7 %custom-call.39 = f32[2,128,128]{1,2,0:T(8,128)S(1)} custom-call(f32[2,128,128]{2,1,0:T(8,128)S(1)} %get-tuple-element.303), custom_call_target="InvertDiagBlocksLowerTriangular" | custom-call | tf_op jit(solution)/shard_map/while/body/eval_jaxpr/triangular_solve/custom-call.4 | solution.py:34
  402.1 13.6 %psum.45 = f32[256,4]{0,1:T(4,128)S(1)} all-reduce(f32[256,4]{0,1:T(4,128)S(1)} %fusion.105), channel_id=1, replica_groups=mesh['section'=4,'row'=8] {'row'}, use_global_device_ids=true, to_apply=%region_8.8 | all-reduce | flops 1024 | bytes 8192 | tf_op jit(solution)/shard_map/while/body/eval_jaxpr/psum | solution.py:57
  418.2 4.3 collective-permute-start
  425.0 13.6 %psum.40 = f32[256,4]{0,1:T(4,128)S(1)} all-reduce(f32[256,4]{0,1:T(4,128)S(1)} %fusion.46), channel_id=1, replica_groups=mesh['section'=4,'row'=8] {'row'}, use_global_device_ids=true, to_apply=%region_10.13 | all-reduce | flops 1024 | bytes 8192 | tf_op jit(solution)/shard_map/psum | solution.py:57
  442.1 11.0 %psum.41 = f32[4,256]{1,0:T(4,128)S(1)} all-reduce(f32[4,256]{1,0:T(4,128)S(1)} %fusion.17), channel_id=1, replica_groups=mesh['section'=4,'row'=8] {'section'}, use_global_device_ids=true, to_apply=%region_11.14 | all-reduce | flops 1024 | bytes 8192 | tf_op jit(solution)/shard_map/psum | solution.py:25
  453.2 13.6 %psum.42 = f32[4,4]{0,1:T(4,128)S(1)} all-reduce(f32[4,4]{0,1:T(4,128)S(1)} %fusion.47), channel_id=1, replica_groups=mesh['section'=4,'row'=8] {'row'}, use_global_device_ids=true, to_apply=%region_12.15 | all-reduce | flops 16 | bytes 128 | tf_op jit(solution)/shard_map/psum | solution.py:83
  (130 shorter events, 53.3 us)
Async XLA Ops:
  7.2 87.4 %copy-start = (bf16[1024,256]{1,0:T(8,128)(2,1)S(1)}, bf16[1024,256]{1,0:T(8,128)(2,1)}, u32[]{:S(2)}) copy-start(bf16[1024,256]{1,0:T(8,128)(2,1)} %param.10) | copy-start | bytes 1572868
  7.2 84.1 %copy-start.1 = (bf16[512,1024]{1,0:T(8,128)(2,1)S(1)}, bf16[512,1024]{1,0:T(8,128)(2,1)}, u32[]{:S(2)}) copy-start(bf16[512,1024]{1,0:T(8,128)(2,1)} %param.9) | copy-start | bytes 3145732
  7.2 126.1 %reduce-scatter.8.cloned.1.call-start = ((), (), s32[]{:S(2)}) async-start(), calls=%async_computation.3 | async-start | bytes 2359296 | tf_op jit(solution)/shard_map/reduce_scatter | solution.py:42
  7.2 27.3 %collective-permute-start.1 = (bf16[512,1024]{1,0:T(8,128)(2,1)}, bf16[512,1024]{1,0:T(8,128)(2,1)S(1)}, u32[]{:S(2)}, u32[]{:S(2)}) collective-permute-start(bf16[512,1024]{1,0:T(8,128)(2,1)} %param.9), channel_id=1, source_target_pairs={{0,8},{8,16},{16,24},{24,0},{1,9},{9,17},{17,25},{25,1},{2,10},{10... | collective-permute-start | bytes 3145736 | tf_op jit(solution)/shard_map/ppermute | solution.py:11
  34.6 25.3 %collective-permute-start.2 = (bf16[512,1024]{1,0:T(8,128)(2,1)S(1)}, bf16[512,1024]{1,0:T(8,128)(2,1)}, u32[]{:S(2)}, u32[]{:S(2)}) collective-permute-start(bf16[512,1024]{1,0:T(8,128)(2,1)S(1)} %collective-permute-done.1), channel_id=1, source_target_pairs={{0,8},{8,16},{16,24},{24,0},{1,9},{9,17},{17,25},{25,1},{2,10},{10... | collective-permute-start | bytes 3145736 | tf_op jit(solution)/shard_map/ppermute | solution.py:11
  59.9 24.7 %collective-permute-start.3 = (bf16[512,1024]{1,0:T(8,128)(2,1)}, bf16[512,1024]{1,0:T(8,128)(2,1)}, u32[]{:S(2)}, u32[]{:S(2)}) collective-permute-start(bf16[512,1024]{1,0:T(8,128)(2,1)} %collective-permute-done.2), channel_id=1, source_target_pairs={{0,8},{8,16},{16,24},{24,0},{1,9},{9,17},{17,25},{25,1},{2,10},{10... | collective-permute-start | bytes 3145736 | tf_op jit(solution)/shard_map/ppermute | solution.py:11
  91.2 6.2 %copy-start.4 = (bf16[4,1024]{1,0:T(4,128)(2,1)S(1)}, bf16[4,1024]{1,0:T(4,128)(2,1)}, u32[]{:S(2)}) copy-start(bf16[4,1024]{1,0:T(4,128)(2,1)} %param.11) | copy-start | bytes 24580
  91.3 3.2 copy-start.2
  97.3 69.5 %reduce-scatter.10.cloned.1.call-start = ((), (), s32[]{:S(2)}) async-start(), calls=%async_computation.5 | async-start | bytes 1179648
  102.1 120.6 %all-reduce.3.cloned.1.call-start = ((), (), s32[]{:S(2)}) async-start(), calls=%async_computation.4 | async-start | bytes 524288 | tf_op jit(solution)/shard_map/psum | solution.py:52
  135.7 333.2 %reduce-scatter.12.cloned.1.call-start = ((), (), s32[]{:S(2)}) async-start(), calls=%async_computation.6 | async-start | bytes 655360
  325.8 4.7 collective-permute-start
  371.6 5.5 %collective-permute-start = (f32[4,256]{1,0:T(4,128)S(1)}, f32[4,256]{1,0:T(4,128)S(1)}, u32[]{:S(2)}, u32[]{:S(2)}) collective-permute-start(f32[4,256]{1,0:T(4,128)S(1)} %fusion.110), channel_id=1, source_target_pairs={{0,8},{8,16},{16,24},{1,9},{9,17},{17,25},{2,10},{10,18},{18,26},{... | collective-permute-start | bytes 12296 | tf_op jit(solution)/shard_map/while/body/eval_jaxpr/ppermute | solution.py:20
  418.2 5.6 %collective-permute-start = (f32[4,256]{1,0:T(4,128)S(1)}, f32[4,256]{1,0:T(4,128)S(1)}, u32[]{:S(2)}, u32[]{:S(2)}) collective-permute-start(f32[4,256]{1,0:T(4,128)S(1)} %fusion.110), channel_id=1, source_target_pairs={{0,8},{8,16},{16,24},{1,9},{9,17},{17,25},{2,10},{10,18},{18,26},{... | collective-permute-start | bytes 12296 | tf_op jit(solution)/shard_map/while/body/eval_jaxpr/ppermute | solution.py:20
  439.7 31.0 %copy-start.3 = (f32[4,256]{1,0:T(4,128)}, f32[4,256]{1,0:T(4,128)S(1)}, u32[]{:S(2)}) copy-start(f32[4,256]{1,0:T(4,128)S(1)} %bitcast_select_fusion.1) | copy-start | bytes 12292
Sparse Core Ops, SparseCore 0:
  97.4 35.8 reduce-scatter.7
  135.6 31.1 reduce-scatter.9
  169.1 53.5 all-reduce.2
  441.0 25.7 reduce-scatter.11
